TPU v7x, 128 devices: a whole 4x4x4 slice. The times are simulated.
128 devices in a mesh: worker: 16 (over y, z), mp: 8 (over x, core).
Axes of the slice: x: 4, y: 4, z: 4, core: 2. Of those that a mesh axis runs over, the one named last changes fastest.
Arguments:
- gradients: bfloat16 [256, 2097152], P('worker', 'mp'), may hold values from -30 to 30
- center: float32 [2097152], P('mp'), may hold values from -6 to 6
- outside_sq: float32 [3, 256], P(None, 'worker'), may hold values from 419430.4 to 4194304
- radius: float32 [3], replicated, may hold values from 1.5 to 3
Outputs:
- new_center: float32 [2097152], P('mp')
- norms: float32 [256], P('worker')
All inputs are finite; a program needn't handle non-finite values.
Results may differ from a plain program's by a relative error of at most 0.0003.
Values sent between devices are 32-bit elements; how exact they have to be, the bound alone decides.
A program may use at most 64 MiB of HBM per device.

v0:
```python
import jax
import jax.numpy as jnp
from jax import lax
from jax.sharding import PartitionSpec as P

ITERS = 3


def copy_for_each(value, axis):
    peers = lax.axis_size(axis)
    return lax.all_to_all(
        jnp.broadcast_to(value[None], (peers, *value.shape)), axis, 0, 0, tiled=True
    )


def taken_together(value, axis):
    everything = copy_for_each(value, axis)
    return jnp.sum(everything, axis=0)


def split_up(value, dim, peers):
    dims = value.shape
    tiles = value.reshape(*dims[:dim], peers, dims[dim] // peers, *dims[dim + 1 :])
    return jnp.moveaxis(tiles, dim, 0)


def sent_and_summed(value, axis, dim):
    tiles = split_up(value, dim, lax.axis_size(axis))
    arrived = lax.all_to_all(tiles, axis, split_axis=0, concat_axis=0, tiled=True)
    return arrived.sum(axis=0)


def in_order(tiles, dim):
    dims = list(tiles.shape[1:])
    dims[dim] *= tiles.shape[0]
    return jnp.moveaxis(tiles, 0, dim).reshape(dims)


def collect(value, axis, dim):
    tiles = copy_for_each(value, axis)
    return in_order(tiles, dim)


def shards(gradients, center, outside_sq, radius):
    workers_all = gradients.shape[0] * lax.axis_size("worker")
    root_total = jnp.sqrt(jnp.float32(center.shape[0] * lax.axis_size("mp")))
    share_len = center.shape[0] // lax.axis_size("worker")
    value = center
    norms = jnp.zeros((gradients.shape[0],), jnp.float32)
    for step in range(ITERS):
        diff = gradients.astype(jnp.float32) - value[None, :]
        partial_value = jnp.sum(diff * diff, axis=1)
        squared = taken_together(partial_value, "mp") + outside_sq[step]
        norms = jnp.sqrt(squared)
        factor = jnp.minimum(jnp.float32(1.0), radius[step] * root_total / norms)
        local = jnp.sum(factor[:, None] * diff, axis=0)
        share = sent_and_summed(local, "worker", 0)
        offset = lax.axis_index("worker") * share_len
        mine = lax.dynamic_slice_in_dim(value, offset, share_len, 0)
        updated = mine + share / jnp.float32(workers_all)
        value = collect(updated, "worker", 0)
    return (value, norms)


def solution(mesh):
    placed = (P("worker", "mp"), P("mp"), P(None, "worker"), P())
    return jax.shard_map(
        shards, mesh=mesh, in_specs=placed, out_specs=(P("mp"), P("worker")), check_vma=False
    )
```

profile of v0, /device:TPU:0, one launch (start us, length us, event | category | flops | bytes accessed | tf_op | source)
XLA Modules:
  0.0 215.0 jit_solution(793448960033494886)
XLA Ops:
  0.6 0.0 copy-start
  0.6 0.0 copy-start.1
  0.7 0.0 copy-start.2
  0.7 5.5 %fusion.10 = f32[16]{0:T(128)S(1)} fusion(bf16[16,262144]{1,0:T(8,128)(2,1)} %param.4, f32[262144]{0:T(1024)} %param.5), kind=kLoop, calls=%fused_computation.13 | loop fusion | flops 16777200 | bytes 9437248 | tf_op jit(solution)/shard_map/reduce_sum | solution.py:52
  6.2 0.6 broadcast_in_dim.12
  6.8 4.4 %all-to-all-start = ((f32[8,1,16]{2,1,0:T(1,128)}), f32[8,1,16]{2,1,0:T(1,128)S(1)}, u32[]{:S(2)}, u32[]{:S(2)}) async-start(f32[8,1,16]{2,1,0:T(1,128)} %broadcast_in_dim.12), calls=%async_computation | async-start | bytes 8192 | tf_op jit(solution)/shard_map/all_to_all | solution.py:11
  11.2 0.0 copy-done.1
  11.2 0.7 fusion.19
  12.4 4.0 %all-to-all-done = f32[8,1,16]{2,1,0:T(1,128)S(1)} async-done(((f32[8,1,16]{2,1,0:T(1,128)}), f32[8,1,16]{2,1,0:T(1,128)S(1)}, u32[]{:S(2)}, u32[]{:S(2)}) %all-to-all-start) | async-done | bytes 544 | tf_op jit(solution)/shard_map/all_to_all | solution.py:11
  16.4 0.0 copy-done.2
  16.5 0.0 copy-done
  16.5 14.0 %fusion.11 = f32[262144]{0:T(1024)} fusion(bf16[16,262144]{1,0:T(8,128)(2,1)} %param.4, f32[16]{0:T(128)S(1)} %fusion.16, f32[262144]{0:T(1024)S(1)} %copy-done), kind=kLoop, calls=%fused_computation.14 | loop fusion | flops 16515072 | bytes 10485824 | tf_op jit(solution)/shard_map/reduce_sum | solution.py:56
  30.5 8.0 %all-to-all-start.1 = ((f32[16,1,16384]{2,1,0:T(1,128)}), f32[16,1,16384]{2,1,0:T(1,128)S(1)}, u32[]{:S(2)}, u32[]{:S(2)}) async-start(f32[16,1,16384]{2,1,0:T(1,128)} %bitcast.3), calls=%async_computation.1 | async-start | bytes 2097152 | tf_op jit(solution)/shard_map/all_to_all | solution.py:29
  38.5 17.7 %all-to-all-done.1 = f32[16,1,16384]{2,1,0:T(1,128)S(1)} async-done(((f32[16,1,16384]{2,1,0:T(1,128)}), f32[16,1,16384]{2,1,0:T(1,128)S(1)}, u32[]{:S(2)}, u32[]{:S(2)}) %all-to-all-start.1) | async-done | bytes 1048608 | tf_op jit(solution)/shard_map/all_to_all | solution.py:29
  56.2 0.7 reduce_sum.111
  57.0 0.8 broadcast_in_dim.13
  57.8 18.7 %all_to_all.63 = f32[16,1,16384]{2,1,0:T(1,128)S(1)} all-to-all(f32[16,1,16384]{2,1,0:T(1,128)S(1)} %broadcast_in_dim.13), channel_id=1, replica_groups=mesh['worker'=16,'mp'=8] {'worker'}, dimensions={0} | all-to-all | bytes 2097152 | tf_op jit(solution)/shard_map/all_to_all | solution.py:11
  76.5 5.2 %fusion.8 = f32[16]{0:T(128)S(1)} fusion(bf16[16,262144]{1,0:T(8,128)(2,1)} %param.4, f32[262144]{0:T(1024)S(1)} %bitcast.37), kind=kLoop, calls=%fused_computation.11 | loop fusion | flops 16777200 | bytes 9437248 | tf_op jit(solution)/shard_map/reduce_sum | solution.py:52
  81.6 0.6 broadcast_in_dim.14
  82.2 3.3 %all-to-all-start.3 = ((f32[8,1,16]{2,1,0:T(1,128)}), f32[8,1,16]{2,1,0:T(1,128)S(1)}, u32[]{:S(2)}, u32[]{:S(2)}) async-start(f32[8,1,16]{2,1,0:T(1,128)} %broadcast_in_dim.14), calls=%async_computation.3 | async-start | bytes 8192 | tf_op jit(solution)/shard_map/all_to_all | solution.py:11
  86.2 4.5 %all-to-all-done.3 = f32[8,1,16]{2,1,0:T(1,128)S(1)} async-done(((f32[8,1,16]{2,1,0:T(1,128)}), f32[8,1,16]{2,1,0:T(1,128)S(1)}, u32[]{:S(2)}, u32[]{:S(2)}) %all-to-all-start.3) | async-done | bytes 544 | tf_op jit(solution)/shard_map/all_to_all | solution.py:11
  90.7 13.0 %fusion.9 = f32[262144]{0:T(1024)S(1)} fusion(bf16[16,262144]{1,0:T(8,128)(2,1)} %param.4, f32[16]{0:T(128)S(1)} %fusion.17, f32[262144]{0:T(1024)S(1)} %bitcast.38), kind=kLoop, calls=%fused_computation.12 | loop fusion | flops 16515072 | bytes 10485824 | tf_op jit(solution)/shard_map/reduce_sum | solution.py:56
  103.7 20.2 %all_to_all.64 = f32[16,1,16384]{2,1,0:T(1,128)S(1)} all-to-all(f32[16,1,16384]{2,1,0:T(1,128)S(1)} %bitcast.41), channel_id=1, replica_groups=mesh['worker'=16,'mp'=8] {'worker'}, dimensions={0} | all-to-all | bytes 2097152 | tf_op jit(solution)/shard_map/all_to_all | solution.py:29
  123.9 0.7 reduce_sum.115
  124.6 0.8 broadcast_in_dim.15
  125.4 19.6 %all_to_all.65 = f32[16,1,16384]{2,1,0:T(1,128)S(1)} all-to-all(f32[16,1,16384]{2,1,0:T(1,128)S(1)} %broadcast_in_dim.15), channel_id=1, replica_groups=mesh['worker'=16,'mp'=8] {'worker'}, dimensions={0} | all-to-all | bytes 2097152 | tf_op jit(solution)/shard_map/all_to_all | solution.py:11
  145.0 5.2 %fusion.6 = f32[16]{0:T(128)S(1)} fusion(bf16[16,262144]{1,0:T(8,128)(2,1)} %param.4, f32[262144]{0:T(1024)S(1)} %bitcast.34), kind=kLoop, calls=%fused_computation.9 | loop fusion | flops 16777200 | bytes 9437248 | tf_op jit(solution)/shard_map/reduce_sum | solution.py:52
  150.2 0.6 broadcast_in_dim.16
  150.8 3.5 %all-to-all-start.6 = ((f32[8,1,16]{2,1,0:T(1,128)}), f32[8,1,16]{2,1,0:T(1,128)S(1)}, u32[]{:S(2)}, u32[]{:S(2)}) async-start(f32[8,1,16]{2,1,0:T(1,128)} %broadcast_in_dim.16), calls=%async_computation.6 | async-start | bytes 8192 | tf_op jit(solution)/shard_map/all_to_all | solution.py:11
  155.0 4.3 %all-to-all-done.6 = f32[8,1,16]{2,1,0:T(1,128)S(1)} async-done(((f32[8,1,16]{2,1,0:T(1,128)}), f32[8,1,16]{2,1,0:T(1,128)S(1)}, u32[]{:S(2)}, u32[]{:S(2)}) %all-to-all-start.6) | async-done | bytes 544 | tf_op jit(solution)/shard_map/all_to_all | solution.py:11
  159.2 0.5 fusion.18
  159.8 13.0 %fusion.7 = f32[262144]{0:T(1024)S(1)} fusion(bf16[16,262144]{1,0:T(8,128)(2,1)} %param.4, f32[16]{0:T(128)S(1)} %get-tuple-element.3, f32[262144]{0:T(1024)S(1)} %bitcast.35), kind=kLoop, calls=%fused_computation.10 | loop fusion | flops 16515072 | bytes 10485824 | tf_op jit(solution)/shard_map/reduce_sum | solution.py:56
  172.8 20.1 %all_to_all.66 = f32[16,1,16384]{2,1,0:T(1,128)S(1)} all-to-all(f32[16,1,16384]{2,1,0:T(1,128)S(1)} %bitcast.42), channel_id=1, replica_groups=mesh['worker'=16,'mp'=8] {'worker'}, dimensions={0} | all-to-all | bytes 2097152 | tf_op jit(solution)/shard_map/all_to_all | solution.py:29
  192.8 0.7 reduce_sum.119
  193.6 0.8 broadcast_in_dim.17
  194.4 19.6 %all_to_all.67 = f32[16,1,16384]{2,1,0:T(1,128)S(1)} all-to-all(f32[16,1,16384]{2,1,0:T(1,128)S(1)} %broadcast_in_dim.17), channel_id=1, replica_groups=mesh['worker'=16,'mp'=8] {'worker'}, dimensions={0} | all-to-all | bytes 2097152 | tf_op jit(solution)/shard_map/all_to_all | solution.py:11
  214.0 1.0 copy.16
  (8 shorter events, 0.1 us)
Async XLA Ops:
  0.6 15.8 %copy-start = (f32[262144]{0:T(1024)S(1)}, f32[262144]{0:T(1024)}, u32[]{:S(2)}) copy-start(f32[262144]{0:T(1024)} %param.5) | copy-start | bytes 3145732
  0.6 10.6 %copy-start.1 = (f32[3]{0:T(128)S(1)}, f32[3]{0:T(128)}, u32[]{:S(2)}) copy-start(f32[3]{0:T(128)} %param.7) | copy-start | bytes 40
  0.7 15.8 %copy-start.2 = (f32[3,16]{1,0:T(4,128)S(1)}, f32[3,16]{1,0:T(4,128)}, u32[]{:S(2)}) copy-start(f32[3,16]{1,0:T(4,128)} %param.6) | copy-start | bytes 580
  6.8 9.6 %all-to-all-start = ((f32[8,1,16]{2,1,0:T(1,128)}), f32[8,1,16]{2,1,0:T(1,128)S(1)}, u32[]{:S(2)}, u32[]{:S(2)}) async-start(f32[8,1,16]{2,1,0:T(1,128)} %broadcast_in_dim.12), calls=%async_computation | async-start | bytes 8192 | tf_op jit(solution)/shard_map/all_to_all | solution.py:11
  30.5 25.8 %all-to-all-start.1 = ((f32[16,1,16384]{2,1,0:T(1,128)}), f32[16,1,16384]{2,1,0:T(1,128)S(1)}, u32[]{:S(2)}, u32[]{:S(2)}) async-start(f32[16,1,16384]{2,1,0:T(1,128)} %bitcast.3), calls=%async_computation.1 | async-start | bytes 2097152 | tf_op jit(solution)/shard_map/all_to_all | solution.py:29
  82.2 8.5 %all-to-all-start.3 = ((f32[8,1,16]{2,1,0:T(1,128)}), f32[8,1,16]{2,1,0:T(1,128)S(1)}, u32[]{:S(2)}, u32[]{:S(2)}) async-start(f32[8,1,16]{2,1,0:T(1,128)} %broadcast_in_dim.14), calls=%async_computation.3 | async-start | bytes 8192 | tf_op jit(solution)/shard_map/all_to_all | solution.py:11
  150.8 8.5 %all-to-all-start.6 = ((f32[8,1,16]{2,1,0:T(1,128)}), f32[8,1,16]{2,1,0:T(1,128)S(1)}, u32[]{:S(2)}, u32[]{:S(2)}) async-start(f32[8,1,16]{2,1,0:T(1,128)} %broadcast_in_dim.16), calls=%async_computation.6 | async-start | bytes 8192 | tf_op jit(solution)/shard_map/all_to_all | solution.py:11
where the time goes:
time: 216 us; the launch traced here: 215 us
  blocking collectives  98.1 us (45%)
  other arithmetic  58.5 us (27%)
  waiting for transfers between devices  30.5 us (14%)
  starting transfers between devices  19.3 us (9%)
  local copies, waits for them, and re-layouts  5.93 us (3%)
  between operations  2.69 us (1%)
    all_to_all x3, blocking collectives, copy_for_each(): lax.all_to_all(jnp.broadcast_to(value[None], (peers, *value.shape)), axis...  57.9 us
    all_to_all x2, blocking collectives, sent_and_summed(): lax.all_to_all(tiles, axis, split_axis=0, concat_axis=0, tiled=True)  40.3 us
    reduce_sum x3, other arithmetic, shards(): local = jnp.sum(factor[:, None] * diff, axis=0)  39.9 us
    all_to_all x1, waiting for transfers between devices, sent_and_summed(): lax.all_to_all(tiles, axis, split_axis=0, concat_axis=0, tiled=True)  17.7 us
    reduce_sum x3, other arithmetic, shards(): partial_value = jnp.sum(diff * diff, axis=1)  15.9 us
    all_to_all x3, waiting for transfers between devices, copy_for_each(): lax.all_to_all(jnp.broadcast_to(value[None], (peers, *value.shape)), axis...  12.7 us
    all_to_all x3, starting transfers between devices, copy_for_each(): lax.all_to_all(jnp.broadcast_to(value[None], (peers, *value.shape)), axis...  11.2 us
    all_to_all x1, starting transfers between devices, sent_and_summed(): lax.all_to_all(tiles, axis, split_axis=0, concat_axis=0, tiled=True)  8.05 us
  transfers between devices with their start and end apart: 4, of which 4 were waited for; matrix products, arithmetic and copies ran while one was open for 0% of the time, Pallas kernels for 0%

commit v1 on v0

v1 whole, which is shorter than its diff:
```python
import jax
import jax.numpy as jnp
from jax import lax
from jax.experimental import pallas as pl
from jax.experimental.pallas import tpu as pltpu
from jax.sharding import PartitionSpec as P

ITERS = 3
SIDE = 4
LANES = 128
TILE = 32
LOADS = 16
MESH = pl.DeviceIdType.MESH


def kernel(
    workers_all, root_total, peers,
    radius_ref, grads_hbm, center_hbm, outside_ref,
    out_ref, norms_ref,
    grads, value, local, first, second, second_out, sums, weights,
    load_sem, center_sem, sum_send, sum_recv,
    first_send, first_recv, second_send, second_recv,
    third_send, third_recv, fourth_send, fourth_recv,
):
    workers = grads.shape[0]
    rows = value.shape[1]
    half_rows = rows // 2
    block = half_rows // (SIDE * SIDE)
    chunk = block * SIDE
    per_load = rows // LOADS
    worker = lax.axis_index("worker")
    part = lax.axis_index("mp")
    at = (lax.div(worker, SIDE), lax.rem(worker, SIDE))

    def turned(place, by):
        return lax.rem(place + by, SIDE)

    def device(half, along, across):
        spots = [None, None]
        spots[half] = turned(at[half], along)
        spots[1 - half] = turned(at[1 - half], across)
        return {"worker": spots[0] * SIDE + spots[1], "mp": part}

    def rows_of(half, along, across):
        start = half * half_rows + turned(at[half], along) * chunk + turned(at[1 - half], across) * block
        return pl.ds(pl.multiple_of(start, block), block)

    def send(src, dst, send_sem, recv_sem, to):
        return pltpu.make_async_remote_copy(
            src_ref=src, dst_ref=dst, send_sem=send_sem, recv_sem=recv_sem,
            device_id=to, device_id_type=MESH,
        )

    center_copy = pltpu.make_async_copy(center_hbm, value.at[0], center_sem)
    center_copy.start()

    def load(i):
        columns = pl.ds(i * per_load * LANES, per_load * LANES)
        return pltpu.make_async_copy(grads_hbm.at[:, columns], grads.at[:, columns], load_sem.at[i])

    for i in range(LOADS):
        load(i).start()

    barrier = pltpu.get_barrier_semaphore()
    greeted = 0
    for half in range(2):
        for by in range(1, SIDE):
            pl.semaphore_signal(barrier, 1, device_id=device(half, by, 0), device_id_type=MESH)
            greeted += 1
    for by in range(1, peers):
        pl.semaphore_signal(
            barrier, 1, device_id={"worker": worker, "mp": lax.rem(part + by, peers)}, device_id_type=MESH
        )
        greeted += 1

    def squares(step, start, count, totals):
        for k in range(count):
            columns = pl.ds(pl.multiple_of((start + k) * LANES, LANES), LANES)
            diff = grads[:, columns].astype(jnp.float32) - value[step, pl.ds(start + k, 1), :]
            totals = (totals[1], totals[0] + diff * diff)
        return totals

    def squares_of(step, start, count, totals):
        return lax.fori_loop(
            0, count // TILE,
            lambda i, t: squares(step, pl.multiple_of(start + i * TILE, TILE), TILE, t), totals,
        )

    zero = jnp.zeros((workers, LANES), jnp.float32)
    totals = (zero, zero)
    center_copy.wait()
    for i in range(LOADS):
        load(i).wait()
        totals = squares_of(0, i * per_load, per_load, totals)

    pl.semaphore_wait(barrier, greeted)

    own_lane = lax.broadcasted_iota(jnp.int32, (workers, LANES), 1) % workers == lax.broadcasted_iota(
        jnp.int32, (workers, LANES), 0
    )
    own_row = lax.broadcasted_iota(
        jnp.int32, (TILE // 2, 2 * LANES), 1
    ) // workers == lax.broadcasted_iota(jnp.int32, (TILE // 2, 2 * LANES), 0)

    def factors(step, totals):
        each = jnp.sum(totals[0] + totals[1], axis=1, keepdims=True)
        mine = jnp.sum(jnp.where(own_lane, each, 0.0), axis=0, keepdims=True)
        sums[step, pl.ds(part, 1), :] = mine
        copies = []
        for by in range(1, peers):
            copies.append(send(
                sums.at[step, pl.ds(part, 1)], sums.at[step, pl.ds(part, 1)],
                sum_send.at[step, by - 1], sum_recv.at[step, by - 1],
                {"worker": worker, "mp": lax.rem(part + by, peers)},
            ))
        for copy in copies:
            copy.start()
        for copy in copies:
            copy.wait_recv()
        norms = jnp.sqrt(jnp.sum(sums[step], axis=0, keepdims=True) + outside_ref[step : step + 1, :])
        factor = jnp.minimum(1.0, radius_ref[step] * root_total / norms)
        high = factor.astype(jnp.bfloat16).astype(jnp.float32)
        low = (factor - high).astype(jnp.bfloat16).astype(jnp.float32)
        for i, term in enumerate((high, low)):
            wide = jnp.broadcast_to(jnp.concatenate([term, term], axis=1), own_row.shape)
            weights[i * (TILE // 2) : (i + 1) * (TILE // 2), :] = jnp.where(own_row, wide, 0.0).astype(jnp.bfloat16)
        whole = jnp.sum(high + low, axis=1, keepdims=True) * (workers / LANES)
        return norms, whole, copies

    def weigh(step, start, whole):
        for i in range(block // TILE):
            base = pl.multiple_of(start + i * TILE, TILE)
            stacks = []
            for side in range(2):
                stacks.append(jnp.concatenate([
                    grads[:, pl.ds(pl.multiple_of((base + side * (TILE // 2) + j) * LANES, LANES), LANES)]
                    for j in range(TILE // 2)
                ], axis=0))
            both = jnp.dot(weights[...], jnp.concatenate(stacks, axis=1), preferred_element_type=jnp.float32)
            both = both[: TILE // 2] + both[TILE // 2 :]
            for side in range(2):
                here = pl.ds(pl.multiple_of(base + side * (TILE // 2), TILE // 2), TILE // 2)
                local[here, :] = both[:, side * LANES : (side + 1) * LANES] - whole * value[step, here, :]

    order = (1, 2, 3, 0)
    reach = (2, 1, 3)

    for step in range(ITERS):
        norms, whole, pending = factors(step, totals)
        if step == ITERS - 1:
            norms_ref[...] = norms

        def first_copy(half, along, across):
            here = rows_of(half, along, across)
            at_start = pl.multiple_of(turned(at[1 - half], across) * block, block)
            return send(
                local.at[here], first.at[step, half, along - 1, pl.ds(at_start, block)],
                first_send.at[half, along - 1, across], first_recv.at[step, half, along - 1, across],
                device(half, along, 0),
            )

        def spread(i, carry):
            across = lax.rem(i + 1, SIDE)
            for along in reach + (0,):
                for half in range(2):
                    here = rows_of(half, along, across)
                    weigh(step, here.start, whole)
                    if along:
                        first_copy(half, along, across).start()
            return carry

        lax.fori_loop(0, SIDE, spread, 0)

        def second_copy(half, across):
            return send(
                second_out.at[half, across - 1], second.at[step, half, across - 1],
                second_send.at[half, across - 1], second_recv.at[step, half, across - 1],
                device(half, 0, across),
            )

        kept = [None, None]
        for across in order:
            for half in range(2):
                at_start = pl.multiple_of(turned(at[1 - half], across) * block, block)
                total = local[rows_of(half, 0, across), :]
                for along in range(1, SIDE):
                    first_copy(half, along, across).wait_recv()
                    total = total + first[step, half, along - 1, pl.ds(at_start, block), :]
                if across:
                    second_out[half, across - 1] = total
                    second_copy(half, across).start()
                else:
                    local[rows_of(half, 0, 0), :] = total

        def third_copy(half, across):
            here = rows_of(half, 0, 0)
            return send(
                value.at[step + 1, here], value.at[step + 1, here],
                third_send.at[half, across - 1], third_recv.at[step, half, across - 1],
                device(half, 0, across),
            )

        def fourth_copy(half, along, across):
            here = rows_of(half, 0, SIDE - across)
            return send(
                value.at[step + 1, here], value.at[step + 1, here],
                fourth_send.at[half, along - 1, across], fourth_recv.at[step, half, along - 1, across],
                device(half, along, 0),
            )

        for half in range(2):
            here = rows_of(half, 0, 0)
            total = local[here, :]
            for across in range(1, SIDE):
                second_copy(half, across).wait_recv()
                total = total + second[step, half, across - 1]
            value[step + 1, here, :] = value[step, here, :] + total / workers_all
            for across in reach:
                third_copy(half, across).start()
            for along in reach:
                fourth_copy(half, along, 0).start()

        totals = (zero, zero)

        def taken(half, along, across, totals):
            if step == ITERS - 1:
                return totals
            return squares_of(step + 1, rows_of(half, along, across).start, block, totals)

        for half in range(2):
            totals = taken(half, 0, 0, totals)
        for across in (1, 3, 2):
            for half in range(2):
                third_copy(half, across).wait_recv()
                for along in reach:
                    fourth_copy(half, along, across).start()
                totals = taken(half, 0, SIDE - across, totals)
        for across in (0, 1, 3, 2):
            for along in (1, 3, 2):
                for half in range(2):
                    fourth_copy(half, along, across).wait_recv()
                    totals = taken(half, SIDE - along, SIDE - across, totals)

        for copy in pending:
            copy.wait_send()
        for half in range(2):
            for across in range(SIDE):
                for along in range(1, SIDE):
                    first_copy(half, along, across).wait_send()
                    fourth_copy(half, along, across).wait_send()
            for across in range(1, SIDE):
                second_copy(half, across).wait_send()
                third_copy(half, across).wait_send()

    out_ref[...] = value[ITERS]


def shards(gradients, center, outside_sq, radius):
    workers, length = gradients.shape
    rows = length // LANES
    peers = lax.axis_size("mp")
    workers_all = workers * lax.axis_size("worker")
    root_total = float(length * peers) ** 0.5
    half_rows = rows // 2
    block = half_rows // (SIDE * SIDE)
    chunk = block * SIDE

    def body(*refs):
        kernel(float(workers_all), root_total, peers, *refs)

    dma = pltpu.SemaphoreType.DMA
    center_out, norms = pl.pallas_call(
        body,
        out_shape=(
            jax.ShapeDtypeStruct((rows, LANES), jnp.float32),
            jax.ShapeDtypeStruct((1, LANES), jnp.float32),
        ),
        in_specs=[
            pl.BlockSpec(memory_space=pltpu.SMEM),
            pl.BlockSpec(memory_space=pl.ANY),
            pl.BlockSpec(memory_space=pl.ANY),
            pl.BlockSpec(memory_space=pltpu.VMEM),
        ],
        out_specs=(pl.BlockSpec(memory_space=pltpu.VMEM), pl.BlockSpec(memory_space=pltpu.VMEM)),
        scratch_shapes=[
            pltpu.VMEM((workers, length), jnp.bfloat16),
            pltpu.VMEM((ITERS + 1, rows, LANES), jnp.float32),
            pltpu.VMEM((rows, LANES), jnp.float32),
            pltpu.VMEM((ITERS, 2, SIDE - 1, chunk, LANES), jnp.float32),
            pltpu.VMEM((ITERS, 2, SIDE - 1, block, LANES), jnp.float32),
            pltpu.VMEM((2, SIDE - 1, block, LANES), jnp.float32),
            pltpu.VMEM((ITERS, peers, LANES), jnp.float32),
            pltpu.VMEM((TILE, 2 * LANES), jnp.bfloat16),
            dma((LOADS,)),
            dma(()),
            dma((ITERS, peers - 1)),
            dma((ITERS, peers - 1)),
            dma((2, SIDE - 1, SIDE)),
            dma((ITERS, 2, SIDE - 1, SIDE)),
            dma((2, SIDE - 1)),
            dma((ITERS, 2, SIDE - 1)),
            dma((2, SIDE - 1)),
            dma((ITERS, 2, SIDE - 1)),
            dma((2, SIDE - 1, SIDE)),
            dma((ITERS, 2, SIDE - 1, SIDE)),
        ],
        compiler_params=pltpu.CompilerParams(
            collective_id=0, has_side_effects=True, vmem_limit_bytes=48 * 1024 * 1024
        ),
    )(
        radius,
        gradients,
        center.reshape(rows, LANES),
        jnp.tile(outside_sq, (1, LANES // workers)),
    )
    return center_out.reshape(length), norms[0, :workers]


def solution(mesh):
    placed = (P("worker", "mp"), P("mp"), P(None, "worker"), P())
    return jax.shard_map(
        shards, mesh=mesh, in_specs=placed, out_specs=(P("mp"), P("worker")), check_vma=False
    )
```

time: 216 us -> 93.8 us (0.43)
  blocking collectives: 98.1 us -> 0 us
  Pallas kernels: 0 us -> 88.8 us
  other arithmetic: 58.5 us -> 0 us
  waiting for transfers between devices: 30.5 us -> 0 us
  starting transfers between devices: 19.3 us -> 0 us
    all_to_all x5 -> x0, blocking collectives: 98.1 us -> none  [the longest x3 57.9 us: copy_for_each(): lax.all_to_all(jnp.broadcast_to(value[None], (peers, *value.shape)), axis...]
    pallas_call x0 -> x1, Pallas kernels: none -> 88.8 us  [shards(): pl.pallas_call(body, out_shape=(jax.ShapeDtypeStruct((rows, LANES), jnp.f...]
    reduce_sum x12 -> x0, other arithmetic: 57.9 us -> none  [the longest x3 39.9 us: shards(): local = jnp.sum(factor[:, None] * diff, axis=0)]
    all_to_all x4 -> x0, waiting for transfers between devices: 30.5 us -> none  [the longest x1 17.7 us: sent_and_summed(): lax.all_to_all(tiles, axis, split_axis=0, concat_axis=0, tiled=True)]
    all_to_all x4 -> x0, starting transfers between devices: 19.3 us -> none  [the longest x3 11.2 us: copy_for_each(): lax.all_to_all(jnp.broadcast_to(value[None], (peers, *value.shape)), axis...]
    broadcast_in_dim x6 -> x0, local copies, waits for them, and re-layouts: 4.21 us -> none  [copy_for_each(): jnp.broadcast_to(value[None], (peers, *value.shape))]
  transfers between devices with their start and end apart: 4 -> 0, of which waited for: 4 -> 0; matrix products, arithmetic and copies ran while one was open for 0% -> 0% of each run, Pallas kernels for 0% -> 0%
where the time goes in v1:
time: 93.8 us; the launch traced here: 93.6 us
  Pallas kernels  88.8 us (95%)
  local copies, waits for them, and re-layouts  4.2 us (4%)
    pallas_call x1, Pallas kernels, shards(): pl.pallas_call(body, out_shape=(jax.ShapeDtypeStruct((rows, LANES), jnp.f...  88.8 us
    unnamed x5, local copies, waits for them, and re-layouts  2.92 us

profile of v1, /device:TPU:0, one launch (start us, length us, event | category | flops | bytes accessed | tf_op | source)
XLA Modules:
  0.0 93.6 jit_solution(4400655661617515569)
XLA Ops:
  0.6 0.7 tile.4
  1.3 0.1 tile.10.refs_3_
  1.4 0.0 copy-start
  1.4 1.2 %copy-done = f32[262144]{0:T(1024)S(1)} copy-done((f32[262144]{0:T(1024)S(1)}, f32[262144]{0:T(1024)}, u32[]{:S(2)}) %copy-start) | copy-done | bytes 1048600
  2.6 0.0 copy-start.1
  2.6 0.7 copy-done.1
  3.3 88.8 %shard_map.59 = (f32[2048,128]{1,0:T(8,128)S(1)}, f32[1,128]{1,0:T(1,128)S(1)}) custom-call(f32[3]{0:T(128)S(1)} %copy-done.1, bf16[16,262144]{1,0:T(8,128)(2,1)} %refs_1_.1, f32[2048,128]{1,0:T(8,128)S(1)} %bitcast.5, f32[3,128]{1,0:T(4,128)S(1)} %tile.10.refs_3_), custom_call_target="tpu_custom_call" | custom-call | tf_op jit(solution)/shard_map/pallas_call | solution.py:272
  92.1 0.5 slice_bitcast_fusion
  92.6 1.0 %copy.7 = f32[262144]{0:T(1024)} copy(f32[262144]{0:T(1024)S(1)} %bitcast.4) | data formatting | bytes 2097152
Async XLA Ops:
  1.4 1.2 %copy-start = (f32[262144]{0:T(1024)S(1)}, f32[262144]{0:T(1024)}, u32[]{:S(2)}) copy-start(f32[262144]{0:T(1024)} %param.5) | copy-start | bytes 3145732
  2.6 0.7 copy-start.1

commit v2 on v1

v2 whole, which is shorter than its diff:
```python
import jax
import jax.numpy as jnp
from jax import lax
from jax.experimental import pallas as pl
from jax.experimental.pallas import tpu as pltpu
from jax.sharding import PartitionSpec as P

ITERS = 3
SIDE = 4
LANES = 128
GROUPS = 2
LOADS = 16
MESH = pl.DeviceIdType.MESH


def kernel(
    workers_all, root_total, peers,
    radius_hbm, grads_hbm, center_hbm, outside_hbm,
    out_ref, norms_ref,
    radius, outside, grads, value, local, first, second, second_out, sums, weights,
    small_sem, load_sem, center_sem, sum_send, sum_recv,
    first_send, first_recv, second_send, second_recv,
    third_send, third_recv, fourth_send, fourth_recv,
):
    workers = grads.shape[0]
    rows = value.shape[1]
    half_rows = rows // 2
    block = half_rows // (SIDE * SIDE)
    chunk = block * SIDE
    sub = block // GROUPS
    stacks = sub // workers
    per_load = rows // LOADS
    worker = lax.axis_index("worker")
    part = lax.axis_index("mp")
    at = (lax.div(worker, SIDE), lax.rem(worker, SIDE))

    def turned(place, by):
        return lax.rem(place + by, SIDE)

    def device(half, along, across):
        spots = [None, None]
        spots[half] = turned(at[half], along)
        spots[1 - half] = turned(at[1 - half], across)
        return {"worker": spots[0] * SIDE + spots[1], "mp": part}

    def rows_of(half, along, across, group):
        start = half * half_rows + turned(at[half], along) * chunk + turned(at[1 - half], across) * block
        return pl.ds(pl.multiple_of(start + group * sub, sub), sub)

    def send(src, dst, send_sem, recv_sem, to):
        return pltpu.make_async_remote_copy(
            src_ref=src, dst_ref=dst, send_sem=send_sem, recv_sem=recv_sem,
            device_id=to, device_id_type=MESH,
        )

    def load(i):
        here = pl.ds(i * per_load, per_load)
        columns = pl.ds(i * per_load * LANES, per_load * LANES)
        return (
            pltpu.make_async_copy(center_hbm.at[here], value.at[0, here], center_sem.at[i]),
            pltpu.make_async_copy(grads_hbm.at[:, columns], grads.at[:, columns], load_sem.at[i]),
        )

    for i in range(LOADS):
        for copy in load(i):
            copy.start()
    small = (
        pltpu.make_async_copy(radius_hbm, radius, small_sem.at[0]),
        pltpu.make_async_copy(outside_hbm, outside, small_sem.at[1]),
    )
    for copy in small:
        copy.start()

    barrier = pltpu.get_barrier_semaphore()
    greeted = 0
    for half in range(2):
        for by in range(1, SIDE):
            pl.semaphore_signal(barrier, 1, device_id=device(half, by, 0), device_id_type=MESH)
            greeted += 1
    for by in range(1, peers):
        pl.semaphore_signal(
            barrier, 1, device_id={"worker": worker, "mp": lax.rem(part + by, peers)}, device_id_type=MESH
        )
        greeted += 1

    def squares(step, start, count, totals):
        for k in range(count):
            columns = pl.ds(pl.multiple_of((start + k) * LANES, LANES), LANES)
            diff = grads[:, columns].astype(jnp.float32) - value[step, pl.ds(start + k, 1), :]
            totals = (totals[1], totals[0] + diff * diff)
        return totals

    def squares_of(step, start, count, totals):
        return lax.fori_loop(
            0, count // 32,
            lambda i, t: squares(step, pl.multiple_of(start + i * 32, 32), 32, t), totals,
        ) if count > 32 else squares(step, start, count, totals)

    own_lane = lax.broadcasted_iota(jnp.int32, (workers, LANES), 1) % workers == lax.broadcasted_iota(
        jnp.int32, (workers, LANES), 0
    )
    own_row = lax.broadcasted_iota(
        jnp.int32, (workers, 2 * LANES), 1
    ) // workers == lax.broadcasted_iota(jnp.int32, (workers, 2 * LANES), 0)

    zero = jnp.zeros((workers, LANES), jnp.float32)
    totals = (zero, zero)
    for i in range(LOADS):
        for copy in load(i):
            copy.wait()
        totals = squares_of(0, i * per_load, per_load, totals)
    for copy in small:
        copy.wait()
    elsewhere = jnp.concatenate([outside[...]] * (LANES // workers), axis=1)

    pl.semaphore_wait(barrier, greeted)

    def factors(step, totals, pending):
        each = jnp.sum(totals[0] + totals[1], axis=1, keepdims=True)
        mine = jnp.sum(jnp.where(own_lane, each, 0.0), axis=0, keepdims=True)
        sums[step, pl.ds(part, 1), :] = mine
        copies = []
        for by in range(1, peers):
            copies.append(send(
                sums.at[step, pl.ds(part, 1)], sums.at[step, pl.ds(part, 1)],
                sum_send.at[step, by - 1], sum_recv.at[step, by - 1],
                {"worker": worker, "mp": lax.rem(part + by, peers)},
            ))
        for copy in copies:
            copy.start()
        for copy in pending:
            copy.wait_send()
        for copy in copies:
            copy.wait_recv()
        norms = jnp.sqrt(jnp.sum(sums[step], axis=0, keepdims=True) + elsewhere[step : step + 1, :])
        factor = jnp.minimum(1.0, radius[step] * root_total / norms)
        high = factor.astype(jnp.bfloat16).astype(jnp.float32)
        low = (factor - high).astype(jnp.bfloat16).astype(jnp.float32)
        for i, term in enumerate((high, low)):
            wide = jnp.broadcast_to(jnp.concatenate([term, term], axis=1), own_row.shape)
            weights[i * workers : (i + 1) * workers, :] = jnp.where(own_row, wide, 0.0).astype(jnp.bfloat16)
        whole = jnp.sum(high + low, axis=1, keepdims=True) * (workers / LANES)
        return norms, whole, copies

    def weigh(step, start, whole):
        columns = []
        for i in range(stacks):
            columns.append(jnp.concatenate([
                grads[:, pl.ds(pl.multiple_of((start + i * workers + j) * LANES, LANES), LANES)]
                for j in range(workers)
            ], axis=0))
        both = jnp.dot(weights[...], jnp.concatenate(columns, axis=1), preferred_element_type=jnp.float32)
        both = both[:workers] + both[workers:]
        for i in range(stacks):
            here = pl.ds(pl.multiple_of(start + i * workers, workers), workers)
            local[here, :] = both[:, i * LANES : (i + 1) * LANES] - whole * value[step, here, :]

    reach = (2, 1, 3)

    pending = []
    for step in range(ITERS):
        norms, whole, pending = factors(step, totals, pending)
        if step == ITERS - 1:
            norms_ref[...] = norms

        def first_copy(half, along, across, group):
            here = rows_of(half, along, across, group)
            at_start = pl.multiple_of(turned(at[1 - half], across) * block + group * sub, sub)
            return send(
                local.at[here], first.at[step, half, along - 1, pl.ds(at_start, sub)],
                first_send.at[half, along - 1, across, group], first_recv.at[step, half, along - 1, across, group],
                device(half, along, 0),
            )

        def spread(across, group):
            for along in reach + (0,):
                for half in range(2):
                    weigh(step, rows_of(half, along, across, group).start, whole)
            for along in reach:
                for half in range(2):
                    first_copy(half, along, across, group).start()

        def spread_far(i, carry):
            spread(1 + lax.rem(i, SIDE - 1), lax.div(i, SIDE - 1))
            return carry

        def spread_near(i, carry):
            spread(0, i)
            return carry

        lax.fori_loop(0, (SIDE - 1) * GROUPS, spread_far, 0)
        lax.fori_loop(0, GROUPS, spread_near, 0)

        def second_copy(half, across, group):
            return send(
                second_out.at[half, across - 1, group], second.at[step, half, across - 1, group],
                second_send.at[half, across - 1, group], second_recv.at[step, half, across - 1, group],
                device(half, 0, across),
            )

        def summed(half, across, group):
            at_start = pl.multiple_of(turned(at[1 - half], across) * block + group * sub, sub)
            total = local[rows_of(half, 0, across, group), :]
            for along in reach:
                first_copy(half, along, across, group).wait_recv()
                total = total + first[step, half, along - 1, pl.ds(at_start, sub), :]
            return total

        def third_copy(half, across, group):
            here = rows_of(half, 0, 0, group)
            return send(
                value.at[step + 1, here], value.at[step + 1, here],
                third_send.at[half, across - 1, group], third_recv.at[step, half, across - 1, group],
                device(half, 0, across),
            )

        def fourth_copy(half, along, across, group):
            here = rows_of(half, 0, SIDE - across, group)
            return send(
                value.at[step + 1, here], value.at[step + 1, here],
                fourth_send.at[half, along - 1, across, group], fourth_recv.at[step, half, along - 1, across, group],
                device(half, along, 0),
            )

        for group in range(GROUPS):
            for across in range(1, SIDE):
                for half in range(2):
                    second_out[half, across - 1, group] = summed(half, across, group)
                    second_copy(half, across, group).start()

        for group in range(GROUPS):
            for half in range(2):
                here = rows_of(half, 0, 0, group)
                total = summed(half, 0, group)
                for across in range(1, SIDE):
                    second_copy(half, across, group).wait_recv()
                    total = total + second[step, half, across - 1, group]
                value[step + 1, here, :] = value[step, here, :] + total / workers_all
                for across in reach:
                    third_copy(half, across, group).start()
                for along in reach:
                    fourth_copy(half, along, 0, group).start()

        totals = (zero, zero)

        def taken(half, along, across, group, totals):
            if step == ITERS - 1:
                return totals
            return squares_of(step + 1, rows_of(half, along, across, group).start, sub, totals)

        for group in range(GROUPS):
            for half in range(2):
                totals = taken(half, 0, 0, group, totals)
        for group in range(GROUPS):
            for across in (1, 3, 2):
                for half in range(2):
                    third_copy(half, across, group).wait_recv()
                    for along in reach:
                        fourth_copy(half, along, across, group).start()
                    totals = taken(half, 0, SIDE - across, group, totals)
        for group in range(GROUPS):
            for across in (0, 1, 3, 2):
                for along in (1, 3, 2):
                    for half in range(2):
                        fourth_copy(half, along, across, group).wait_recv()
                        totals = taken(half, SIDE - along, SIDE - across, group, totals)

        pending += [
            copy
            for group in range(GROUPS)
            for half in range(2)
            for copy in [
                make(half, along, across, group)
                for make in (first_copy, fourth_copy) for along in range(1, SIDE) for across in range(SIDE)
            ] + [make(half, across, group) for make in (second_copy, third_copy) for across in range(1, SIDE)]
        ]

    for copy in pending:
        copy.wait_send()
    out_ref[...] = value[ITERS]


def shards(gradients, center, outside_sq, radius):
    workers, length = gradients.shape
    rows = length // LANES
    peers = lax.axis_size("mp")
    workers_all = workers * lax.axis_size("worker")
    root_total = float(length * peers) ** 0.5
    half_rows = rows // 2
    block = half_rows // (SIDE * SIDE)
    chunk = block * SIDE
    sub = block // GROUPS

    def body(*refs):
        kernel(float(workers_all), root_total, peers, *refs)

    dma = pltpu.SemaphoreType.DMA
    center_out, norms = pl.pallas_call(
        body,
        out_shape=(
            jax.ShapeDtypeStruct((rows, LANES), jnp.float32),
            jax.ShapeDtypeStruct((1, LANES), jnp.float32),
        ),
        in_specs=[
            pl.BlockSpec(memory_space=pltpu.HBM),
            pl.BlockSpec(memory_space=pltpu.HBM),
            pl.BlockSpec(memory_space=pltpu.HBM),
            pl.BlockSpec(memory_space=pltpu.HBM),
        ],
        out_specs=(pl.BlockSpec(memory_space=pltpu.VMEM), pl.BlockSpec(memory_space=pltpu.VMEM)),
        scratch_shapes=[
            pltpu.SMEM((ITERS,), jnp.float32),
            pltpu.VMEM((ITERS, workers), jnp.float32),
            pltpu.VMEM((workers, length), jnp.bfloat16),
            pltpu.VMEM((ITERS + 1, rows, LANES), jnp.float32),
            pltpu.VMEM((rows, LANES), jnp.float32),
            pltpu.VMEM((ITERS, 2, SIDE - 1, chunk, LANES), jnp.float32),
            pltpu.VMEM((ITERS, 2, SIDE - 1, GROUPS, sub, LANES), jnp.float32),
            pltpu.VMEM((2, SIDE - 1, GROUPS, sub, LANES), jnp.float32),
            pltpu.VMEM((ITERS, peers, LANES), jnp.float32),
            pltpu.VMEM((2 * workers, 2 * LANES), jnp.bfloat16),
            dma((2,)),
            dma((LOADS,)),
            dma((LOADS,)),
            dma((ITERS, peers - 1)),
            dma((ITERS, peers - 1)),
            dma((2, SIDE - 1, SIDE, GROUPS)),
            dma((ITERS, 2, SIDE - 1, SIDE, GROUPS)),
            dma((2, SIDE - 1, GROUPS)),
            dma((ITERS, 2, SIDE - 1, GROUPS)),
            dma((2, SIDE - 1, GROUPS)),
            dma((ITERS, 2, SIDE - 1, GROUPS)),
            dma((2, SIDE - 1, SIDE, GROUPS)),
            dma((ITERS, 2, SIDE - 1, SIDE, GROUPS)),
        ],
        compiler_params=pltpu.CompilerParams(
            collective_id=0, has_side_effects=True, vmem_limit_bytes=48 * 1024 * 1024
        ),
    )(*(
        pltpu.with_memory_space_constraint(value, pltpu.HBM)
        for value in (radius, gradients, center.reshape(rows, LANES), outside_sq)
    ))
    return center_out.reshape(length), norms[0, :workers]


def solution(mesh):
    placed = (P("worker", "mp"), P("mp"), P(None, "worker"), P())
    return jax.shard_map(
        shards, mesh=mesh, in_specs=placed, out_specs=(P("mp"), P("worker")), check_vma=False
    )
```

time: 93.8 us -> 86.4 us (0.921)
  Pallas kernels: 88.8 us -> 84.1 us
  local copies, waits for them, and re-layouts: 4.2 us -> 1.55 us
    pallas_call x1, Pallas kernels: 88.8 us -> 84.1 us  [shards(): pl.pallas_call(body, out_shape=(jax.ShapeDtypeStruct((rows, LANES), jnp.f...]
    unnamed x5 -> x1, local copies, waits for them, and re-layouts: 2.92 us -> 1.04 us
where the time goes in v2:
time: 86.4 us; the launch traced here: 86.3 us
  Pallas kernels  84.1 us (97%)
  local copies, waits for them, and re-layouts  1.55 us (2%)
    pallas_call x1, Pallas kernels, shards(): pl.pallas_call(body, out_shape=(jax.ShapeDtypeStruct((rows, LANES), jnp.f...  84.1 us

profile of v2, /device:TPU:0, one launch (start us, length us, event | category | flops | bytes accessed | tf_op | source)
XLA Modules:
  0.0 86.3 jit_solution(10726905085350112540)
XLA Ops:
  0.6 84.1 %shard_map.59 = (f32[2048,128]{1,0:T(8,128)S(1)}, f32[1,128]{1,0:T(1,128)S(1)}) custom-call(f32[3]{0:T(128)} %refs_0_.1, bf16[16,262144]{1,0:T(8,128)(2,1)} %refs_1_.1, f32[2048,128]{1,0:T(8,128)} %bitcast.5, f32[3,16]{1,0:T(4,128)} %refs_3_.1), custom_call_target="tpu_custom_call" | custom-call | tf_op jit(solution)/shard_map/pallas_call | solution.py:298
  84.7 0.5 slice_bitcast_fusion
  85.2 1.0 %copy.7 = f32[262144]{0:T(1024)} copy(f32[262144]{0:T(1024)S(1)} %bitcast.4) | data formatting | bytes 2097152

commit v3 on v2

--- a/solution.py
+++ b/solution.py
@@ -84,9 +84,9 @@
         greeted += 1
 
     def squares(step, start, count, totals):
+        slab = grads[:, pl.ds(pl.multiple_of(start * LANES, count * LANES), count * LANES)]
         for k in range(count):
-            columns = pl.ds(pl.multiple_of((start + k) * LANES, LANES), LANES)
-            diff = grads[:, columns].astype(jnp.float32) - value[step, pl.ds(start + k, 1), :]
+            diff = slab[:, k * LANES : (k + 1) * LANES].astype(jnp.float32) - value[step, pl.ds(start + k, 1), :]
             totals = (totals[1], totals[0] + diff * diff)
         return totals
 
@@ -143,11 +143,11 @@
         return norms, whole, copies
 
     def weigh(step, start, whole):
+        slab = grads[:, pl.ds(pl.multiple_of(start * LANES, sub * LANES), sub * LANES)]
         columns = []
         for i in range(stacks):
             columns.append(jnp.concatenate([
-                grads[:, pl.ds(pl.multiple_of((start + i * workers + j) * LANES, LANES), LANES)]
-                for j in range(workers)
+                slab[:, (i * workers + j) * LANES : (i * workers + j + 1) * LANES] for j in range(workers)
             ], axis=0))
         both = jnp.dot(weights[...], jnp.concatenate(columns, axis=1), preferred_element_type=jnp.float32)
         both = both[:workers] + both[workers:]
@@ -161,7 +161,7 @@
     for step in range(ITERS):
         norms, whole, pending = factors(step, totals, pending)
         if step == ITERS - 1:
-            norms_ref[...] = norms
+            norms_ref[...] = norms[0, :workers]
 
         def first_copy(half, along, across, group):
             here = rows_of(half, along, across, group)
@@ -280,6 +280,17 @@
     out_ref[...] = value[ITERS]
 
 
+def write_out(center_ref, norms_ref, center_out, norms_out, sem):
+    copies = (
+        pltpu.make_async_copy(center_ref, center_out, sem.at[0]),
+        pltpu.make_async_copy(norms_ref, norms_out, sem.at[1]),
+    )
+    for copy in copies:
+        copy.start()
+    for copy in copies:
+        copy.wait()
+
+
 def shards(gradients, center, outside_sq, radius):
     workers, length = gradients.shape
     rows = length // LANES
@@ -299,7 +310,7 @@
         body,
         out_shape=(
             jax.ShapeDtypeStruct((rows, LANES), jnp.float32),
-            jax.ShapeDtypeStruct((1, LANES), jnp.float32),
+            jax.ShapeDtypeStruct((workers,), jnp.float32),
         ),
         in_specs=[
             pl.BlockSpec(memory_space=pltpu.HBM),
@@ -340,7 +351,18 @@
         pltpu.with_memory_space_constraint(value, pltpu.HBM)
         for value in (radius, gradients, center.reshape(rows, LANES), outside_sq)
     ))
-    return center_out.reshape(length), norms[0, :workers]
+    center_out, norms = pl.pallas_call(
+        write_out,
+        out_shape=(
+            jax.ShapeDtypeStruct((rows, LANES), jnp.float32),
+            jax.ShapeDtypeStruct((workers,), jnp.float32),
+        ),
+        in_specs=[pl.BlockSpec(memory_space=pl.ANY)] * 2,
+        out_specs=(pl.BlockSpec(memory_space=pltpu.HBM),) * 2,
+        scratch_shapes=[dma((2,))],
+        compiler_params=pltpu.CompilerParams(vmem_limit_bytes=1024 * 1024),
+    )(center_out, norms)
+    return center_out.reshape(length), norms
 
 
 def solution(mesh):

time: 86.4 us -> 85.5 us (0.990)
  local copies, waits for them, and re-layouts: 1.55 us -> 0 us
    unnamed x1 -> x0, local copies, waits for them, and re-layouts: 1.04 us -> none
    pallas_call x0 -> x1, Pallas kernels: none -> 0.99 us  [shards(): pl.pallas_call(write_out, out_shape=(jax.ShapeDtypeStruct((rows, LANES),...]
where the time goes in v3:
time: 85.5 us; the launch traced here: 85.4 us
  Pallas kernels  84.8 us (99%)
    pallas_call x1, Pallas kernels, shards(): pl.pallas_call(body, out_shape=(jax.ShapeDtypeStruct((rows, LANES), jnp.f...  83.8 us

profile of v3, /device:TPU:0, one launch (start us, length us, event | category | flops | bytes accessed | tf_op | source)
XLA Modules:
  0.0 85.4 jit_solution(5042162303404270082)
XLA Ops:
  0.6 83.8 %shard_map.59 = (f32[2048,128]{1,0:T(8,128)S(1)}, f32[16]{0:T(128)S(1)}) custom-call(f32[3]{0:T(128)} %refs_0_.1, bf16[16,262144]{1,0:T(8,128)(2,1)} %refs_1_.1, f32[2048,128]{1,0:T(8,128)} %bitcast.2, f32[3,16]{1,0:T(4,128)} %refs_3_.1), custom_call_target="tpu_custom_call" | custom-call | tf_op jit(solution)/shard_map/pallas_call | solution.py:309
  84.4 1.0 %shard_map.60 = (f32[2048,128]{1,0:T(8,128)}, f32[16]{0:T(128)}) custom-call(f32[2048,128]{1,0:T(8,128)S(1)} %get-tuple-element.6.center_ref, f32[16]{0:T(128)S(1)} %get-tuple-element.7.norms_ref), custom_call_target="tpu_custom_call" | custom-call | tf_op jit(solution)/shard_map/pallas_call | solution.py:354

commit v4 on v3

--- a/solution.py
+++ b/solution.py
@@ -6,6 +6,7 @@
 from jax.sharding import PartitionSpec as P
 
 ITERS = 3
+FAR = (2, 3, 1)
 SIDE = 4
 LANES = 128
 GROUPS = 2
@@ -181,7 +182,7 @@
                     first_copy(half, along, across, group).start()
 
         def spread_far(i, carry):
-            spread(1 + lax.rem(i, SIDE - 1), lax.div(i, SIDE - 1))
+            spread(1 + lax.rem(i + 1, SIDE - 1), lax.div(i, SIDE - 1))
             return carry
 
         def spread_near(i, carry):
@@ -223,7 +224,7 @@
             )
 
         for group in range(GROUPS):
-            for across in range(1, SIDE):
+            for across in FAR:
                 for half in range(2):
                     second_out[half, across - 1, group] = summed(half, across, group)
                     second_copy(half, across, group).start()

time: 85.5 us -> 85.5 us (level)
  no operation moved by 1% of the time
where the time goes in v4:
time: 85.5 us; the launch traced here: 85.4 us
  Pallas kernels  84.7 us (99%)
    pallas_call x1, Pallas kernels, shards(): pl.pallas_call(body, out_shape=(jax.ShapeDtypeStruct((rows, LANES), jnp.f...  83.7 us

profile of v4, /device:TPU:0, one launch (start us, length us, event | category | flops | bytes accessed | tf_op | source)
XLA Modules:
  0.0 85.4 jit_solution(2472131163991268039)
XLA Ops:
  0.6 83.7 %shard_map.59 = (f32[2048,128]{1,0:T(8,128)S(1)}, f32[16]{0:T(128)S(1)}) custom-call(f32[3]{0:T(128)} %refs_0_.1, bf16[16,262144]{1,0:T(8,128)(2,1)} %refs_1_.1, f32[2048,128]{1,0:T(8,128)} %bitcast.2, f32[3,16]{1,0:T(4,128)} %refs_3_.1), custom_call_target="tpu_custom_call" | custom-call | tf_op jit(solution)/shard_map/pallas_call | solution.py:310
  84.4 1.0 %shard_map.60 = (f32[2048,128]{1,0:T(8,128)}, f32[16]{0:T(128)}) custom-call(f32[2048,128]{1,0:T(8,128)S(1)} %get-tuple-element.6.center_ref, f32[16]{0:T(128)S(1)} %get-tuple-element.7.norms_ref), custom_call_target="tpu_custom_call" | custom-call | tf_op jit(solution)/shard_map/pallas_call | solution.py:355

commit v5 on v4

--- a/solution.py
+++ b/solution.py
@@ -261,7 +261,7 @@
                     totals = taken(half, 0, SIDE - across, group, totals)
         for group in range(GROUPS):
             for across in (0, 1, 3, 2):
-                for along in (1, 3, 2):
+                for along in (2, 1, 3):
                     for half in range(2):
                         fourth_copy(half, along, across, group).wait_recv()
                         totals = taken(half, SIDE - along, SIDE - across, group, totals)

time: 85.5 us -> 85 us (level)
  no operation moved by 1% of the time
where the time goes in v5:
time: 85 us; the launch traced here: 84.8 us
  Pallas kernels  84.2 us (99%)
    pallas_call x1, Pallas kernels, shards(): pl.pallas_call(body, out_shape=(jax.ShapeDtypeStruct((rows, LANES), jnp.f...  83.2 us

profile of v5, /device:TPU:0, one launch (start us, length us, event | category | flops | bytes accessed | tf_op | source)
XLA Modules:
  0.0 84.8 jit_solution(1747378097677359199)
XLA Ops:
  0.6 83.2 %shard_map.59 = (f32[2048,128]{1,0:T(8,128)S(1)}, f32[16]{0:T(128)S(1)}) custom-call(f32[3]{0:T(128)} %refs_0_.1, bf16[16,262144]{1,0:T(8,128)(2,1)} %refs_1_.1, f32[2048,128]{1,0:T(8,128)} %bitcast.2, f32[3,16]{1,0:T(4,128)} %refs_3_.1), custom_call_target="tpu_custom_call" | custom-call | tf_op jit(solution)/shard_map/pallas_call | solution.py:310
  83.9 1.0 %shard_map.60 = (f32[2048,128]{1,0:T(8,128)}, f32[16]{0:T(128)}) custom-call(f32[2048,128]{1,0:T(8,128)S(1)} %get-tuple-element.6.center_ref, f32[16]{0:T(128)S(1)} %get-tuple-element.7.norms_ref), custom_call_target="tpu_custom_call" | custom-call | tf_op jit(solution)/shard_map/pallas_call | solution.py:355
